TPU v7x, 32 devices: a whole 2x2x4 slice. The times are simulated.
32 devices in a mesh: seq: 8 (over y, x, core), head: 4 (over z).
Axes of the slice: x: 2, y: 2, z: 4, core: 2. Of those that a mesh axis runs over, the one named last changes fastest.
Arguments:
- latent_cache: bfloat16 [2, 16384, 576], P(None, 'seq'), may hold values from -8 to 8
- draft_latent: bfloat16 [2, 64, 576], P(None, 'seq'), may hold values from -9 to 9
- query_nope: bfloat16 [2, 64, 128, 128], P(None, None, 'head'), may hold values from -6 to 6
- query_rope: bfloat16 [2, 64, 128, 64], P(None, None, 'head'), may hold values from -8 to 8
- parents: int32 [2, 64], replicated, may hold values from -1 to 62, as said below
- lengths: int32 [2], replicated, may hold values from 8192 to 16384
- key_weight: bfloat16 [128, 128, 512], P('head'), may hold values from -0.25 to 0.25
- value_weight: bfloat16 [128, 512, 128], P('head'), may hold values from -0.25 to 0.25
- out_weight: bfloat16 [16384, 7168], P('head', 'seq'), may hold values from -0.046875 to 0.046875
- residual: bfloat16 [2, 64, 7168], P(None, None, 'seq'), may hold values from -40 to 40
- norm_gain: bfloat16 [7168], P('seq'), may hold values from 0.5 to 1.5
- vocab_weight: bfloat16 [7168, 8192], P('seq', 'head'), may hold values from -0.21875 to 0.21875
Outputs:
- logits: bfloat16 [2, 64, 8192], P(None, None, ('head', 'seq'))
Inputs may be any that keep to these rules, and one draw needn't show every extreme that they name: `parents`: token 0 is the root of each tree with parent -1; every other token's parent is an earlier token; the last token's parent is the token just before it.
All inputs are finite; a program needn't handle non-finite values.
Results may differ from a plain program's by a relative error of at most 0.02.
Values may be sent and summed in bfloat16 or wider, within the bound.
No kernel may reach another device: no remote copies, remote signals or barrier semaphores. Data moves between devices by JAX's collectives and lax.ppermute only.
A program may use at most 128 MiB of HBM per device.

v0:
```python
import math
import jax
import jax.numpy as jnp
from jax import lax
from jax.sharding import PartitionSpec as P

D = 7168
NEGATIVE = -1e30
EPSILON = 1e-06


def ancestry_of(parents):
    token_count = parents.shape[1]
    indices = jnp.arange(token_count, dtype=jnp.int32)
    linked = (parents[:, :, None] == indices[None, None, :]) | (
        indices[:, None] == indices[None, :]
    )[None]
    reachable = linked.astype(jnp.float32)
    for repeat in range(max(1, (token_count - 1).bit_length())):
        product = jnp.einsum("bij,bjk->bik", reachable, reachable, precision=lax.Precision.HIGHEST)
        reachable = jnp.where(product > 0.5, 1.0, 0.0).astype(jnp.float32)
    return reachable


def per_device(
    latent_cache,
    draft_latent,
    query_nope,
    query_rope,
    parents,
    lengths,
    key_weight,
    value_weight,
    out_weight,
    residual,
    norm_gain,
    vocab_weight,
):
    requests, cache_local, width = latent_cache.shape
    latent = value_weight.shape[1]
    heads_local = key_weight.shape[0]
    drafted = query_nope.shape[1]
    draft_local = draft_latent.shape[1]
    scaling = 1.0 / math.sqrt(query_nope.shape[3] + query_rope.shape[3])
    seat = lax.axis_index("seq")
    absorbed = jnp.einsum(
        "bthn,hnl->bthl", query_nope, key_weight, preferred_element_type=jnp.float32
    ).astype(jnp.bfloat16)
    queries = jnp.concatenate([absorbed, query_rope], axis=-1)
    ancestry = ancestry_of(parents)
    own_tree = lax.dynamic_slice_in_dim(ancestry, seat * draft_local, draft_local, 2)
    positions = seat * cache_local + jnp.arange(cache_local, dtype=jnp.int32)
    live = positions[None, :] < lengths[:, None]
    cache_values = latent_cache[:, :, :latent]
    draft_values = draft_latent[:, :, :latent]
    row_count = drafted * heads_local
    block = queries.reshape(requests, row_count, width)
    tree_block = own_tree
    tree_block = jnp.broadcast_to(
        tree_block[:, :, None, :], (requests, drafted, heads_local, draft_local)
    )
    tree_block = tree_block.reshape(requests, row_count, draft_local)
    cache_scores = (
        jnp.einsum("brc,bkc->brk", block, latent_cache, preferred_element_type=jnp.float32)
        * scaling
    )
    cache_scores = jnp.where(live[:, None, :], cache_scores, NEGATIVE)
    draft_scores = (
        jnp.einsum("brc,bkc->brk", block, draft_latent, preferred_element_type=jnp.float32)
        * scaling
    )
    draft_scores = jnp.where(tree_block > 0.5, draft_scores, NEGATIVE)
    cache_scores, draft_scores, tree_block = (cache_scores, draft_scores, tree_block)
    local_max = jnp.maximum(jnp.max(cache_scores, -1), jnp.max(draft_scores, -1))
    row_max = lax.pmax(local_max, "seq")
    cache_weights = jnp.where(live[:, None, :], jnp.exp(cache_scores - row_max[..., None]), 0.0)
    draft_weights = jnp.where(tree_block > 0.5, jnp.exp(draft_scores - row_max[..., None]), 0.0)
    total = jnp.sum(cache_weights, -1) + jnp.sum(draft_weights, -1)
    mixed = jnp.einsum(
        "brk,bkl->brl",
        cache_weights.astype(jnp.bfloat16),
        cache_values,
        preferred_element_type=jnp.float32,
    )
    mixed = mixed + jnp.einsum(
        "brk,bkl->brl",
        draft_weights.astype(jnp.bfloat16),
        draft_values,
        preferred_element_type=jnp.float32,
    )
    total, mixed = (total, mixed)
    own_total, own_mixed = (
        lax.psum_scatter(total.astype(jnp.bfloat16), "seq", scatter_dimension=1, tiled=True).astype(
            jnp.float32
        ),
        lax.psum_scatter(mixed.astype(jnp.bfloat16), "seq", scatter_dimension=1, tiled=True).astype(
            jnp.float32
        ),
    )
    latent_out = (own_mixed / own_total[..., None]).astype(jnp.bfloat16)
    latent_out = latent_out.reshape(requests, draft_local, heads_local, latent)
    per_head = jnp.einsum(
        "bthl,hlv->bthv", latent_out, value_weight, preferred_element_type=jnp.float32
    ).astype(jnp.bfloat16)
    head_values = per_head.reshape(requests, draft_local, heads_local * value_weight.shape[2])
    attention = jnp.dot(
        lax.all_gather(head_values, "seq", axis=1, tiled=True),
        out_weight,
        preferred_element_type=jnp.float32,
    )
    attention = lax.psum(attention.astype(jnp.bfloat16), "head").astype(jnp.float32)
    hidden = residual.astype(jnp.float32) + attention
    squares = lax.psum(jnp.sum(hidden * hidden, -1), "seq")
    normed = (
        hidden * lax.rsqrt(squares / D + EPSILON)[..., None] * norm_gain.astype(jnp.float32)
    ).astype(jnp.bfloat16)
    partial_logits = jnp.dot(normed, vocab_weight, preferred_element_type=jnp.float32)
    return lax.psum_scatter(
        partial_logits.astype(jnp.bfloat16), "seq", scatter_dimension=2, tiled=True
    )


def solution(mesh):
    in_specs = (
        P(None, "seq", None),
        P(None, "seq", None),
        P(None, None, "head", None),
        P(None, None, "head", None),
        P(),
        P(),
        P("head", None, None),
        P("head", None, None),
        P("head", "seq"),
        P(None, None, "seq"),
        P("seq"),
        P("seq", "head"),
    )
    out_specs = P(None, None, ("head", "seq"))
    return jax.shard_map(
        per_device, mesh=mesh, in_specs=in_specs, out_specs=out_specs, check_vma=False
    )
```

profile of v0, /device:TPU:0, one launch (start us, length us, event | category | flops | bytes accessed | tf_op | source)
XLA Modules:
  0.0 305.8 jit_solution(1082863160173444389)
XLA Ops:
  6.5 0.0 reduce-scatter.10.cloned.1.call-start
  6.6 1.0 fusion.43
  7.6 0.2 fusion.44
  7.9 0.2 fusion.45
  8.1 0.2 fusion.46
  8.4 0.2 fusion.47
  8.6 0.2 fusion.65
  8.8 0.2 broadcast_in_dim.67
  9.1 0.3 gt.33
  9.4 1.6 copy.41
  11.0 3.4 %fusion.101 = f32[32,512,128]{1,2,0:S(1)} fusion(bf16[32,128,128]{1,2,0:T(8,128)(2,1)S(1)} %bitcast.49, bf16[32,128,512]{2,1,0:T(8,128)(2,1)} %param.18), kind=kOutput, calls=%fused_computation.115 | convolution fusion | flops 536870912 | bytes 13631488
  14.4 0.0 copy-start.1
  14.4 0.7 convert_bitcast_fusion
  15.1 0.6 copy-done.1
  15.7 0.4 copy.42
  16.1 0.0 copy-start.4
  16.1 0.0 copy-start.2
  16.1 0.8 pad_maximum_fusion
  16.9 5.4 %copy.43 = bf16[2,64,32,576]{3,2,1,0:T(8,128)(2,1)} copy(bf16[2,64,32,576]{3,1,0,2:T(8,128)(2,1)S(1)} %pad_maximum_fusion) | data formatting | bytes 9437184 | tf_op jit(solution)/shard_map/concatenate | solution.py:49
  22.4 0.0 copy-done.4
  22.4 0.1 broadcast_compare_fusion
  22.5 0.0 copy-done.2
  22.5 4.0 %fusion.100 = (f32[2,2048]{1,0:T(2,128)S(1)}, f32[2,2048,8]{1,2,0:T(8,128)S(1)}) fusion(pred[2,2048,8]{1,2,0:T(8,128)(4,1)S(1)} %gt.33, bf16[2,2048,576]{2,1,0:T(8,128)(2,1)} %bitcast.47, bf16[2,8,576]{2,1,0:T(8,128)(2,1)S(1)} %copy-done.2), kind=kOutput, calls=%fused_computation.114 | convolution fusion | flops 37842944 | bytes 4917248 | tf_op jit(solution)/shard_map/brc,bkc->brk/dot_general | solution.py:69
  26.4 23.1 %fusion = (f32[2,2048]{1,0:T(2,128)S(1)}, f32[2,2048,2048]{1,2,0:T(8,128)}) fusion(pred[2,2048]{1,0:T(4,128)(4,1)S(1)} %broadcast_compare_fusion, bf16[2,2048,576]{2,1,0:T(8,128)(2,1)} %bitcast.48, bf16[2,2048,576]{1,2,0:T(8,128)(2,1)} %param.12), kind=kOutput, calls=%fused_computation.2 | convolution fusion | flops 9688838144 | bytes 43012096 | tf_op jit(solution)/shard_map/brc,bkc->brk/dot_general | solution.py:64
  49.5 25.5 %pmax.7 = f32[2,2048]{1,0:T(2,128)S(1)} all-reduce(f32[2,2048]{1,0:T(2,128)S(1)} %max.5), channel_id=1, replica_groups=mesh['seq'=8,'head'=4] {'seq'}, use_global_device_ids=true, to_apply=%region_2.3 | all-reduce | flops 4096 | bytes 32768 | tf_op jit(solution)/shard_map/pmax | solution.py:75
  75.1 0.1 fusion.51
  75.2 15.7 %fusion.1 = f32[2,2048]{1,0:T(2,128)S(1)} fusion(f32[2,2048,2048]{1,2,0:T(8,128)} %get-tuple-element.6, f32[2,2048]{1,0:T(2,128)S(1)} %pmax.7, pred[2,2048]{1,0:T(4,128)(4,1)S(1)} %broadcast_compare_fusion), kind=kLoop, calls=%fused_computation.3 | loop fusion | flops 41938944 | bytes 33591296 | tf_op jit(solution)/shard_map/reduce_sum | solution.py:78
  90.9 1.1 copy.82
  91.9 0.0 reduce-scatter.10.cloned.1.call-update
  92.0 0.0 reduce-scatter.6.cloned.1.call-start
  92.0 1.3 fusion.53
  93.3 23.2 %add_convert_fusion = bf16[2,2048,512]{2,1,0:T(8,128)(2,1)} fusion(f32[2,2048,512]{2,1,0:T(8,128)S(1)} %fusion.53, f32[2,2048,2048]{1,2,0:T(8,128)} %get-tuple-element.6, f32[2,2048]{1,0:T(2,128)S(1)} %pmax.7, pred[2,2048]{1,0:T(4,128)(4,1)S(1)} %broadcast_compare_fusion, bf16[2,2048,576]{1,2,0:T(8,128)(2,1)} %param.12), kind=kOutput, calls=%fused_computation.7 | convolution fusion | flops 8636071936 | bytes 50352128 | tf_op jit(solution)/shard_map/brk,bkl->brl/dot_general | solution.py:79
  116.5 0.0 reduce-scatter.6.cloned.1.call-update
  116.5 0.0 all-gather.2.cloned.1.call-start
  116.6 9.0 %reduce-scatter.10.cloned.1.call-done = bf16[256,2]{1,0:T(8,128)(2,1)} async-done(((bf16[2048,2]{1,0:T(8,128)(2,1)}), bf16[256,2]{1,0:T(8,128)(2,1)}) %reduce-scatter.10.cloned.1.call-update) | async-done | bytes 1040
  125.6 0.9 copy.83
  126.5 53.5 %reduce-scatter.6.cloned.1.call-done = bf16[2,256,512]{2,1,0:T(8,128)(2,1)} async-done(((bf16[2,2048,512]{2,1,0:T(8,128)(2,1)}), bf16[2,256,512]{2,1,0:T(8,128)(2,1)}) %reduce-scatter.6.cloned.1.call-update) | async-done | bytes 524304 | tf_op jit(solution)/shard_map/reduce_scatter | solution.py:96
  180.1 1.2 divide_convert_fusion
  181.3 0.0 copy-start.3
  181.3 0.0 copy-start
  181.4 3.1 %fusion.25 = bf16[32,2,1,8,128]{4,3,2,1,0:T(8,128)(2,1)S(1)} fusion(bf16[32,512,128]{2,1,0:T(8,128)(2,1)} %param.19, bf16[2,8,32,512]{3,2,1,0:T(8,128)(2,1)S(1)} %bitcast.50), kind=kOutput, calls=%fused_computation.22 | convolution fusion | flops 67174400 | bytes 4849664 | tf_op jit(solution)/shard_map/bthl,hlv->bthv/dot_general | solution.py:102
  184.4 0.7 copy.89
  185.1 0.0 all-gather.2.cloned.1.call-update
  185.1 0.0 all-reduce.2.cloned.1.call-start
  185.2 23.5 %all-gather.2.cloned.1.call-done = bf16[2,64,4096]{2,1,0:T(8,128)(2,1)} async-done(((bf16[2,8,4096]{2,1,0:T(8,128)(2,1)}), bf16[2,64,4096]{2,1,0:T(8,128)(2,1)}) %all-gather.2.cloned.1.call-update) | async-done | bytes 1048592 | tf_op jit(solution)/shard_map/all_gather | solution.py:107
  208.7 5.4 %fusion.19 = bf16[2,64,896]{2,1,0:T(8,128)(2,1)} fusion(bf16[2,64,4096]{2,1,0:T(8,128)(2,1)} %all-gather.2.cloned.1.call-done, bf16[4096,896]{1,0:T(8,128)(2,1)} %param.20), kind=kOutput, calls=%fused_computation.20 | convolution fusion | flops 939638784 | bytes 8617984 | tf_op jit(solution)/shard_map/dot_general | solution.py:106
  214.1 0.0 all-reduce.2.cloned.1.call-update
  214.1 0.0 reduce-scatter.8.cloned.1.call-start
  214.1 0.0 copy-done.3
  214.1 35.3 %all-reduce.2.cloned.1.call-done = bf16[2,64,896]{2,1,0:T(8,128)(2,1)} async-done(((bf16[2,64,896]{2,1,0:T(8,128)(2,1)}), bf16[2,64,896]{2,1,0:T(8,128)(2,1)}) %all-reduce.2.cloned.1.call-update) | async-done | bytes 229392 | tf_op jit(solution)/shard_map/psum | solution.py:111
  249.4 0.0 copy-done
  249.4 1.1 multiply_reduce_fusion
  250.5 11.8 %psum.15 = f32[2,64]{1,0:T(2,128)S(1)} all-reduce(f32[2,64]{1,0:T(2,128)S(1)} %multiply_reduce_fusion), channel_id=1, replica_groups=mesh['seq'=8,'head'=4] {'seq'}, use_global_device_ids=true, to_apply=%region_9.10 | all-reduce | flops 128 | bytes 1024 | tf_op jit(solution)/shard_map/psum | solution.py:113
  262.3 3.8 %fusion.15 = bf16[2,64,2048]{2,1,0:T(8,128)(2,1)} fusion(bf16[896,2048]{1,0:T(8,128)(2,1)} %param.23, bf16[2,64,896]{2,1,0:T(8,128)(2,1)} %all-reduce.2.cloned.1.call-done, bf16[2,64,896]{2,1,0:T(8,128)(2,1)S(1)} %copy-done, f32[896]{0:T(1024)S(1)} %convert_element_type.66, f32[2,64]{1,0:T(2,128)S(1)} %add_rsqrt_fusion), kind=kOutput, calls=%fused_computation.17 | convolution fusion | flops 470712320 | bytes 4657152 | tf_op jit(solution)/shard_map/dot_general | solution.py:117
  266.1 0.0 reduce-scatter.8.cloned.1.call-update
  266.1 33.1 %reduce-scatter.8.cloned.1.call-done = bf16[2,64,256]{2,1,0:T(8,128)(2,1)} async-done(((bf16[2,64,2048]{2,1,0:T(8,128)(2,1)}), bf16[2,64,256]{2,1,0:T(8,128)(2,1)}) %reduce-scatter.8.cloned.1.call-update) | async-done | bytes 65552 | tf_op jit(solution)/shard_map/reduce_scatter | solution.py:118
  (13 shorter events, 0.2 us)
Async XLA Ops:
  6.5 119.1 %reduce-scatter.10.cloned.1.call-start = ((), (), s32[]{:S(2)}) async-start(), calls=%async_computation.7 | async-start | bytes 589824
  14.4 1.2 copy-start.1
  16.1 6.3 %copy-start.4 = (s32[2]{0:T(128)S(1)}, s32[2]{0:T(128)}, u32[]{:S(2)}) copy-start(s32[2]{0:T(128)} %param.17) | copy-start | bytes 28
  16.1 6.4 %copy-start.2 = (bf16[2,8,576]{2,1,0:T(8,128)(2,1)S(1)}, bf16[2,8,576]{2,1,0:T(8,128)(2,1)}, u32[]{:S(2)}) copy-start(bf16[2,8,576]{2,1,0:T(8,128)(2,1)} %param.13) | copy-start | bytes 55300
  92.0 88.1 %reduce-scatter.6.cloned.1.call-start = ((), (), s32[]{:S(2)}) async-start(), calls=%async_computation.3 | async-start | bytes 4718592 | tf_op jit(solution)/shard_map/reduce_scatter | solution.py:96
  116.5 92.1 %all-gather.2.cloned.1.call-start = ((), (), s32[]{:S(2)}) async-start(), calls=%async_computation.4 | async-start | bytes 1179648 | tf_op jit(solution)/shard_map/all_gather | solution.py:107
  181.3 32.8 %copy-start.3 = (bf16[896]{0:T(1024)(128)(2,1)S(1)}, bf16[896]{0:T(1024)(128)(2,1)}, u32[]{:S(2)}) copy-start(bf16[896]{0:T(1024)(128)(2,1)} %param.22) | copy-start | bytes 5380
  181.3 68.1 %copy-start = (bf16[2,64,896]{2,1,0:T(8,128)(2,1)S(1)}, bf16[2,64,896]{2,1,0:T(8,128)(2,1)}, u32[]{:S(2)}) copy-start(bf16[2,64,896]{2,1,0:T(8,128)(2,1)} %param.21) | copy-start | bytes 688132
  185.1 64.3 %all-reduce.2.cloned.1.call-start = ((), (), s32[]{:S(2)}) async-start(), calls=%async_computation.5 | async-start | bytes 458752 | tf_op jit(solution)/shard_map/psum | solution.py:111
  214.1 85.2 %reduce-scatter.8.cloned.1.call-start = ((), (), s32[]{:S(2)}) async-start(), calls=%async_computation.6 | async-start | bytes 589824 | tf_op jit(solution)/shard_map/reduce_scatter | solution.py:118
Sparse Core Ops, SparseCore 0:
  92.1 33.5 reduce-scatter.9
  129.0 51.0 reduce-scatter.5
  185.3 23.3 all-gather.1
  214.2 35.1 all-reduce.1
  266.2 32.9 reduce-scatter.7
where the time goes:
time: 306 us
  waiting for transfers between devices  155 us (51%)
  matrix products  69.3 us (23%)
  blocking collectives  37.3 us (12%)
  other arithmetic  19.8 us (6%)
  between operations  13.4 us (4%)
  local copies, waits for them, and re-layouts  11.2 us (4%)
    reduce_scatter x1, waiting for transfers between devices, per_device(): lax.psum_scatter(mixed.astype(jnp.bfloat16), 'seq', scatter_dimension=1,...  53.5 us
    psum x1, waiting for transfers between devices, per_device(): lax.psum(attention.astype(jnp.bfloat16), 'head').astype(jnp.float32)  35.3 us
    reduce_scatter x1, waiting for transfers between devices, per_device(): lax.psum_scatter(partial_logits.astype(jnp.bfloat16), 'seq', scatter_dime...  33.1 us
    pmax x1, blocking collectives, per_device(): row_max = lax.pmax(local_max, 'seq')  25.5 us
    all_gather x1, waiting for transfers between devices, per_device(): lax.all_gather(head_values, 'seq', axis=1, tiled=True)  23.5 us
    dot_general x1, matrix products, per_device(): jnp.einsum('brk,bkl->brl', cache_weights.astype(jnp.bfloat16), cache_valu...  23.2 us
    dot_general x1, matrix products, per_device(): jnp.einsum('brc,bkc->brk', block, latent_cache, preferred_element_type=jn...  23.1 us
    reduce_sum x2, other arithmetic, per_device(): total = jnp.sum(cache_weights, -1) + jnp.sum(draft_weights, -1)  15.8 us
  transfers between devices with their start and end apart: 5, of which 5 were waited for; matrix products, arithmetic and copies ran while one was open for 8% of the time, Pallas kernels for 0%

commit v1 on v0

--- a/solution.py
+++ b/solution.py
@@ -108,7 +108,9 @@
         out_weight,
         preferred_element_type=jnp.float32,
     )
-    attention = lax.psum(attention.astype(jnp.bfloat16), "head").astype(jnp.float32)
+    attention = jnp.sum(lax.all_gather(attention.astype(jnp.bfloat16), "head"), axis=0).astype(
+        jnp.float32
+    )
     hidden = residual.astype(jnp.float32) + attention
     squares = lax.psum(jnp.sum(hidden * hidden, -1), "seq")
     normed = (

time: 306 us -> 291 us (0.951)
  waiting for transfers between devices: 155 us -> 120 us
  blocking collectives: 37.3 us -> 58.4 us
    psum x1 -> x0, waiting for transfers between devices: 35.3 us -> none  [per_device(): lax.psum(attention.astype(jnp.bfloat16), 'head').astype(jnp.float32)]
    all_gather x0 -> x1, blocking collectives: none -> 21 us  [per_device(): lax.all_gather(attention.astype(jnp.bfloat16), 'head')]
    unnamed x6 -> x5, waiting for transfers between devices: 9.11 us -> 9.1 us
  transfers between devices with their start and end apart: 5 -> 4, of which waited for: 5 -> 4; matrix products, arithmetic and copies ran while one was open for 8% -> 9% of each run, Pallas kernels for 0% -> 0%
where the time goes in v1:
time: 291 us; the launch traced here: 290 us
  waiting for transfers between devices  120 us (41%)
  matrix products  68.4 us (24%)
  blocking collectives  58.4 us (20%)
  other arithmetic  19 us (7%)
  between operations  13.4 us (5%)
  local copies, waits for them, and re-layouts  11.2 us (4%)
    reduce_scatter x1, waiting for transfers between devices, per_device(): lax.psum_scatter(mixed.astype(jnp.bfloat16), 'seq', scatter_dimension=1,...  53.5 us
    reduce_scatter x1, waiting for transfers between devices, per_device(): lax.psum_scatter(partial_logits.astype(jnp.bfloat16), 'seq', scatter_dime...  33.7 us
    pmax x1, blocking collectives, per_device(): row_max = lax.pmax(local_max, 'seq')  25.5 us
    all_gather x1, waiting for transfers between devices, per_device(): lax.all_gather(head_values, 'seq', axis=1, tiled=True)  23.5 us
    dot_general x1, matrix products, per_device(): jnp.einsum('brk,bkl->brl', cache_weights.astype(jnp.bfloat16), cache_valu...  23.2 us
    dot_general x1, matrix products, per_device(): jnp.einsum('brc,bkc->brk', block, latent_cache, preferred_element_type=jn...  23.1 us
    all_gather x1, blocking collectives, per_device(): lax.all_gather(attention.astype(jnp.bfloat16), 'head')  21 us
    reduce_sum x2, other arithmetic, per_device(): total = jnp.sum(cache_weights, -1) + jnp.sum(draft_weights, -1)  15.8 us
  transfers between devices with their start and end apart: 4, of which 4 were waited for; matrix products, arithmetic and copies ran while one was open for 9% of the time, Pallas kernels for 0%

profile of v1, /device:TPU:0, one launch (start us, length us, event | category | flops | bytes accessed | tf_op | source)
XLA Modules:
  0.0 290.3 jit_solution(8407828024427616928)
XLA Ops:
  6.5 0.0 reduce-scatter.10.cloned.1.call-start
  6.6 1.0 fusion.43
  7.6 0.2 fusion.44
  7.9 0.2 fusion.45
  8.1 0.2 fusion.46
  8.4 0.2 fusion.47
  8.6 0.2 fusion.65
  8.8 0.2 broadcast_in_dim.67
  9.1 0.3 gt.33
  9.4 1.6 copy.41
  11.0 3.4 %fusion.101 = f32[32,512,128]{1,2,0:S(1)} fusion(bf16[32,128,128]{1,2,0:T(8,128)(2,1)S(1)} %bitcast.50, bf16[32,128,512]{2,1,0:T(8,128)(2,1)} %param.18), kind=kOutput, calls=%fused_computation.115 | convolution fusion | flops 536870912 | bytes 13631488
  14.4 0.0 copy-start.1
  14.4 0.7 convert_bitcast_fusion
  15.1 0.6 copy-done.1
  15.7 0.4 copy.42
  16.1 0.0 copy-start.4
  16.1 0.0 copy-start.2
  16.1 0.8 pad_maximum_fusion
  16.9 5.4 %copy.43 = bf16[2,64,32,576]{3,2,1,0:T(8,128)(2,1)} copy(bf16[2,64,32,576]{3,1,0,2:T(8,128)(2,1)S(1)} %pad_maximum_fusion) | data formatting | bytes 9437184 | tf_op jit(solution)/shard_map/concatenate | solution.py:49
  22.4 0.0 copy-done.4
  22.4 0.1 broadcast_compare_fusion
  22.5 0.0 copy-done.2
  22.5 4.0 %fusion.100 = (f32[2,2048]{1,0:T(2,128)S(1)}, f32[2,2048,8]{1,2,0:T(8,128)S(1)}) fusion(pred[2,2048,8]{1,2,0:T(8,128)(4,1)S(1)} %gt.33, bf16[2,2048,576]{2,1,0:T(8,128)(2,1)} %bitcast.48, bf16[2,8,576]{2,1,0:T(8,128)(2,1)S(1)} %copy-done.2), kind=kOutput, calls=%fused_computation.114 | convolution fusion | flops 37842944 | bytes 4917248 | tf_op jit(solution)/shard_map/brc,bkc->brk/dot_general | solution.py:69
  26.4 23.1 %fusion = (f32[2,2048]{1,0:T(2,128)S(1)}, f32[2,2048,2048]{1,2,0:T(8,128)}) fusion(pred[2,2048]{1,0:T(4,128)(4,1)S(1)} %broadcast_compare_fusion, bf16[2,2048,576]{2,1,0:T(8,128)(2,1)} %bitcast.49, bf16[2,2048,576]{1,2,0:T(8,128)(2,1)} %param.12), kind=kOutput, calls=%fused_computation.2 | convolution fusion | flops 9688838144 | bytes 43012096 | tf_op jit(solution)/shard_map/brc,bkc->brk/dot_general | solution.py:64
  49.5 25.5 %pmax.7 = f32[2,2048]{1,0:T(2,128)S(1)} all-reduce(f32[2,2048]{1,0:T(2,128)S(1)} %max.5), channel_id=1, replica_groups=mesh['seq'=8,'head'=4] {'seq'}, use_global_device_ids=true, to_apply=%region_2.3 | all-reduce | flops 4096 | bytes 32768 | tf_op jit(solution)/shard_map/pmax | solution.py:75
  75.1 0.1 fusion.51
  75.2 15.7 %fusion.1 = f32[2,2048]{1,0:T(2,128)S(1)} fusion(f32[2,2048,2048]{1,2,0:T(8,128)} %get-tuple-element.6, f32[2,2048]{1,0:T(2,128)S(1)} %pmax.7, pred[2,2048]{1,0:T(4,128)(4,1)S(1)} %broadcast_compare_fusion), kind=kLoop, calls=%fused_computation.3 | loop fusion | flops 41938944 | bytes 33591296 | tf_op jit(solution)/shard_map/reduce_sum | solution.py:78
  90.9 1.1 copy.82
  91.9 0.0 reduce-scatter.10.cloned.1.call-update
  92.0 0.0 reduce-scatter.6.cloned.1.call-start
  92.0 1.3 fusion.53
  93.3 23.2 %add_convert_fusion = bf16[2,2048,512]{2,1,0:T(8,128)(2,1)} fusion(f32[2,2048,512]{2,1,0:T(8,128)S(1)} %fusion.53, f32[2,2048,2048]{1,2,0:T(8,128)} %get-tuple-element.6, f32[2,2048]{1,0:T(2,128)S(1)} %pmax.7, pred[2,2048]{1,0:T(4,128)(4,1)S(1)} %broadcast_compare_fusion, bf16[2,2048,576]{1,2,0:T(8,128)(2,1)} %param.12), kind=kOutput, calls=%fused_computation.7 | convolution fusion | flops 8636071936 | bytes 50352128 | tf_op jit(solution)/shard_map/brk,bkl->brl/dot_general | solution.py:79
  116.5 0.0 copy-start.3
  116.5 0.0 reduce-scatter.6.cloned.1.call-update
  116.5 0.0 all-gather.3.cloned.1.call-start
  116.6 9.0 %reduce-scatter.10.cloned.1.call-done = bf16[256,2]{1,0:T(8,128)(2,1)} async-done(((bf16[2048,2]{1,0:T(8,128)(2,1)}), bf16[256,2]{1,0:T(8,128)(2,1)}) %reduce-scatter.10.cloned.1.call-update) | async-done | bytes 1040
  125.6 0.9 copy.83
  126.5 53.5 %reduce-scatter.6.cloned.1.call-done = bf16[2,256,512]{2,1,0:T(8,128)(2,1)} async-done(((bf16[2,2048,512]{2,1,0:T(8,128)(2,1)}), bf16[2,256,512]{2,1,0:T(8,128)(2,1)}) %reduce-scatter.6.cloned.1.call-update) | async-done | bytes 524304 | tf_op jit(solution)/shard_map/reduce_scatter | solution.py:96
  180.1 1.2 divide_convert_fusion
  181.3 3.1 %fusion.25 = bf16[32,2,1,8,128]{4,3,2,1,0:T(8,128)(2,1)S(1)} fusion(bf16[32,512,128]{2,1,0:T(8,128)(2,1)} %param.19, bf16[2,8,32,512]{3,2,1,0:T(8,128)(2,1)S(1)} %bitcast.52), kind=kOutput, calls=%fused_computation.22 | convolution fusion | flops 67174400 | bytes 4849664 | tf_op jit(solution)/shard_map/bthl,hlv->bthv/dot_general | solution.py:102
  184.4 0.0 copy-start
  184.4 0.7 copy.89
  185.1 0.0 all-gather.3.cloned.1.call-update
  185.1 0.0 reduce-scatter.8.cloned.1.call-start
  185.1 0.0 copy-done.3
  185.1 23.5 %all-gather.3.cloned.1.call-done = bf16[2,64,4096]{2,1,0:T(8,128)(2,1)} async-done(((bf16[2,8,4096]{2,1,0:T(8,128)(2,1)}), bf16[2,64,4096]{2,1,0:T(8,128)(2,1)}) %all-gather.3.cloned.1.call-update) | async-done | bytes 1048592 | tf_op jit(solution)/shard_map/all_gather | solution.py:107
  208.6 4.7 %fusion.19 = bf16[2,64,896]{2,1,0:T(8,128)(2,1)S(1)} fusion(bf16[2,64,4096]{2,1,0:T(8,128)(2,1)} %all-gather.3.cloned.1.call-done, bf16[4096,896]{1,0:T(8,128)(2,1)} %param.20), kind=kOutput, calls=%fused_computation.20 | convolution fusion | flops 939638784 | bytes 8617984 | tf_op jit(solution)/shard_map/dot_general | solution.py:106
  213.3 21.0 %all-gather = bf16[8,64,896]{2,1,0:T(8,128)(2,1)S(1)} all-gather(bf16[2,64,896]{2,1,0:T(8,128)(2,1)S(1)} %fusion.19), channel_id=2, replica_groups=mesh['seq'=8,'head'=4] {'head'}, dimensions={0}, use_global_device_ids=true | all-gather | bytes 1146880 | tf_op jit(solution)/shard_map/all_gather | solution.py:111
  234.3 0.1 reduce_sum.41
  234.4 0.0 copy-done
  234.5 0.2 multiply_reduce_fusion
  234.6 11.8 %psum.7 = f32[2,64]{1,0:T(2,128)S(1)} all-reduce(f32[2,64]{1,0:T(2,128)S(1)} %multiply_reduce_fusion), channel_id=1, replica_groups=mesh['seq'=8,'head'=4] {'seq'}, use_global_device_ids=true, to_apply=%region_9.10 | all-reduce | flops 128 | bytes 1024 | tf_op jit(solution)/shard_map/psum | solution.py:115
  246.4 3.6 %fusion.15 = bf16[2,64,2048]{2,1,0:T(8,128)(2,1)} fusion(bf16[896,2048]{1,0:T(8,128)(2,1)} %param.23, bf16[2,64,896]{2,1,0:T(8,128)(2,1)S(1)} %reduce_sum.41, bf16[2,64,896]{2,1,0:T(8,128)(2,1)S(1)} %copy-done, f32[896]{0:T(1024)S(1)} %convert_element_type.68, f32[2,64]{1,0:T(2,128)S(1)} %add_rsqrt_fusion), kind=kOutput, calls=%fused_computation.17 | convolution fusion | flops 470712320 | bytes 4657152 | tf_op jit(solution)/shard_map/dot_general | solution.py:119
  250.1 0.0 reduce-scatter.8.cloned.1.call-update
  250.1 33.7 %reduce-scatter.8.cloned.1.call-done = bf16[2,64,256]{2,1,0:T(8,128)(2,1)} async-done(((bf16[2,64,2048]{2,1,0:T(8,128)(2,1)}), bf16[2,64,256]{2,1,0:T(8,128)(2,1)}) %reduce-scatter.8.cloned.1.call-update) | async-done | bytes 65552 | tf_op jit(solution)/shard_map/reduce_scatter | solution.py:120
  (13 shorter events, 0.2 us)
Async XLA Ops:
  6.5 119.1 %reduce-scatter.10.cloned.1.call-start = ((), (), s32[]{:S(2)}) async-start(), calls=%async_computation.6 | async-start | bytes 589824
  14.4 1.2 copy-start.1
  16.1 6.3 %copy-start.4 = (s32[2]{0:T(128)S(1)}, s32[2]{0:T(128)}, u32[]{:S(2)}) copy-start(s32[2]{0:T(128)} %param.17) | copy-start | bytes 28
  16.1 6.4 %copy-start.2 = (bf16[2,8,576]{2,1,0:T(8,128)(2,1)S(1)}, bf16[2,8,576]{2,1,0:T(8,128)(2,1)}, u32[]{:S(2)}) copy-start(bf16[2,8,576]{2,1,0:T(8,128)(2,1)} %param.13) | copy-start | bytes 55300
  92.0 88.1 %reduce-scatter.6.cloned.1.call-start = ((), (), s32[]{:S(2)}) async-start(), calls=%async_computation.3 | async-start | bytes 4718592 | tf_op jit(solution)/shard_map/reduce_scatter | solution.py:96
  116.5 68.6 %copy-start.3 = (bf16[896]{0:T(1024)(128)(2,1)S(1)}, bf16[896]{0:T(1024)(128)(2,1)}, u32[]{:S(2)}) copy-start(bf16[896]{0:T(1024)(128)(2,1)} %param.22) | copy-start | bytes 5380
  116.5 92.1 %all-gather.3.cloned.1.call-start = ((), (), s32[]{:S(2)}) async-start(), calls=%async_computation.4 | async-start | bytes 1179648 | tf_op jit(solution)/shard_map/all_gather | solution.py:107
  184.4 50.1 %copy-start = (bf16[2,64,896]{2,1,0:T(8,128)(2,1)S(1)}, bf16[2,64,896]{2,1,0:T(8,128)(2,1)}, u32[]{:S(2)}) copy-start(bf16[2,64,896]{2,1,0:T(8,128)(2,1)} %param.21) | copy-start | bytes 688132
  185.1 98.7 %reduce-scatter.8.cloned.1.call-start = ((), (), s32[]{:S(2)}) async-start(), calls=%async_computation.5 | async-start | bytes 589824 | tf_op jit(solution)/shard_map/reduce_scatter | solution.py:120
Sparse Core Ops, SparseCore 0:
  92.1 33.5 reduce-scatter.9
  129.0 51.0 reduce-scatter.5
  185.2 23.3 all-gather.2
  250.2 33.5 reduce-scatter.7
